TPU v7x, 32 devices: a whole 2x2x4 slice. The times are simulated.
32 devices in a mesh: gx: 4 (over y, x), gy: 8 (over z, core).
Axes of the slice: x: 2, y: 2, z: 4, core: 2. Of those that a mesh axis runs over, the one named last changes fastest.
Arguments:
- q_nodes: bfloat16 [32, 512, 4096], P(('gx', 'gy')), may hold values from -30 to 30, as said below
- k_cache: bfloat16 [32, 1024, 512], P(('gx', 'gy')), may hold values from -6 to 6, as said below
- v_cache: bfloat16 [32, 1024, 512], P(('gx', 'gy')), may hold values from -6 to 6
- k_tree: bfloat16 [32, 512, 512], P(('gx', 'gy')), may hold values from -6 to 6
- v_tree: bfloat16 [32, 512, 512], P(('gx', 'gy')), may hold values from -6 to 6
- anc_bits: int32 [32, 512, 16], P(('gx', 'gy')), may hold values from -2147483648 to 2147483647, as said below
- node_count: int32 [32], P(('gx', 'gy')), may hold values from 1 to 512, as said below
- cache_len: int32 [32], P(('gx', 'gy')), may hold values from 256 to 1024, as said below
- sinks: float32 [64], replicated, may hold values from 5 to 10
- o_weight: bfloat16 [4096, 2880], P(('gx', 'gy')), may hold values from -0.09375 to 0.09375
Outputs:
- attended: bfloat16 [32, 512, 4096], P(('gx', 'gy'))
- projected: bfloat16 [32, 512, 2880], P(('gx', 'gy'))
Inputs may be any that keep to these rules, and one draw needn't show every extreme that they name: `q_nodes`: custom draw of queries. `k_cache`: custom draw of keys. `anc_bits`: bit j mod 32 of word j // 32 in row i is set exactly when tree node j is node i or one of its ancestors; node 0 is the root and a node's ancestors have lower indices. `node_count`: write request r as a * 8 + b with b < 8. Where a + b is even, the tree has more than (2) * 128 nodes; elsewhere it has at most 128. Request 0 has 512 nodes. `cache_len`: request 0 has 1024 cached positions.
All inputs are finite; a program needn't handle non-finite values.
Results may differ from a plain program's by a relative error of at most 0.0055.
Values may be sent and summed in bfloat16 or wider, within the bound.
A program may use at most 192 MiB of HBM per device.

v0:
```python
import jax
import jax.numpy as jnp
from jax import lax
from jax.sharding import PartitionSpec as P

QH = 64
KVH = 8
HD = 64
BLK = 128


MASKED = -1e30


def passed_along(x, axis, by):
    length = lax.axis_size(axis)
    return lax.ppermute(x, axis, [(i, (i + by) % length) for i in range(length)])


def unpack_bits(bit_words):
    shift_ids = jnp.arange(32, dtype=jnp.int32)
    bit_flags = jnp.bitwise_and(jnp.right_shift(bit_words[:, :, None], shift_ids), 1)
    return bit_flags.reshape(bit_words.shape[0], bit_words.shape[1] * 32) > 0


def attend_rows(
    q_rows, tree_ok, cache_keys, cache_values, tree_keys, tree_values, cache_count, sinks
):
    row_total = q_rows.shape[0]
    groups = QH // KVH
    head_width = groups * HD
    scale_factor = HD ** (-0.5)
    cache_ok = jnp.arange(cache_keys.shape[0], dtype=jnp.int32) < cache_count
    tree_mask = jnp.repeat(tree_ok, groups, axis=0)

    def per_kv_head(kv_head):
        q_part = lax.dynamic_slice_in_dim(q_rows, kv_head * head_width, head_width, 1).reshape(
            row_total * groups, HD
        )
        key_cache = lax.dynamic_slice_in_dim(cache_keys, kv_head * HD, HD, 1)
        value_cache = lax.dynamic_slice_in_dim(cache_values, kv_head * HD, HD, 1)
        key_tree = lax.dynamic_slice_in_dim(tree_keys, kv_head * HD, HD, 1)
        value_tree = lax.dynamic_slice_in_dim(tree_values, kv_head * HD, HD, 1)
        score_cache = (
            jnp.dot(q_part, key_cache.T, preferred_element_type=jnp.float32) * scale_factor
        )
        score_cache = jnp.where(cache_ok[None, :], score_cache, MASKED)
        score_tree = jnp.dot(q_part, key_tree.T, preferred_element_type=jnp.float32) * scale_factor
        score_tree = jnp.where(tree_mask, score_tree, MASKED)
        sink_rows = jnp.tile(
            lax.dynamic_slice_in_dim(sinks, kv_head * groups, groups, 0), row_total
        )
        row_max = jnp.maximum(
            sink_rows, jnp.maximum(jnp.max(score_cache, axis=1), jnp.max(score_tree, axis=1))
        )
        weight_cache = jnp.exp(score_cache - row_max[:, None])
        weight_tree = jnp.exp(score_tree - row_max[:, None])
        denominator = (
            jnp.exp(sink_rows - row_max)
            + jnp.sum(weight_cache, axis=1)
            + jnp.sum(weight_tree, axis=1)
        )
        numerator = jnp.dot(
            weight_cache.astype(jnp.bfloat16), value_cache, preferred_element_type=jnp.float32
        )
        numerator = numerator + jnp.dot(
            weight_tree.astype(jnp.bfloat16), value_tree, preferred_element_type=jnp.float32
        )
        return (numerator / denominator[:, None]).reshape(row_total, head_width)

    per_head = lax.map(per_kv_head, jnp.arange(KVH, dtype=jnp.int32))
    return jnp.transpose(per_head, (1, 0, 2)).reshape(row_total, QH * HD)


def on_device(
    q_nodes, k_cache, v_cache, k_tree, v_tree, anc_bits, node_count, cache_len, sinks, o_weight
):
    queries = q_nodes[0]
    cache_keys = k_cache[0]
    cache_values = v_cache[0]
    tree_keys = k_tree[0]
    tree_values = v_tree[0]
    bit_words = anc_bits[0]
    node_limit = node_count[0]
    cache_count = cache_len[0]
    node_total = queries.shape[0]
    block_size = BLK
    block_count = node_total // block_size
    live_blocks = (node_limit + block_size - 1) // block_size

    def home_step(block_index, result):
        row_start = block_index * block_size
        q_rows = lax.dynamic_slice_in_dim(queries, row_start, block_size, 0)
        bit_rows = lax.dynamic_slice_in_dim(bit_words, row_start, block_size, 0)
        rows_out = attend_rows(
            q_rows,
            unpack_bits(bit_rows),
            cache_keys,
            cache_values,
            tree_keys,
            tree_values,
            cache_count,
            sinks,
        )
        return lax.dynamic_update_slice_in_dim(result, rows_out.astype(jnp.bfloat16), row_start, 0)

    result = jnp.zeros_like(queries)
    send_x = (live_blocks >= block_count - 1).astype(jnp.int32)
    send_y = (live_blocks >= block_count).astype(jnp.int32)
    kept_blocks = live_blocks - send_x - send_y
    start_x = jnp.minimum(kept_blocks, block_count - 1) * block_size
    start_y = jnp.minimum(kept_blocks + send_x, block_count - 1) * block_size
    tree_rows_x = (block_count - 1) * block_size

    def make_parcel(row_start, is_moved, tree_rows):
        q_rows = lax.dynamic_slice_in_dim(queries, row_start, block_size, 0)
        bit_rows = lax.dynamic_slice_in_dim(bit_words, row_start, block_size, 0)
        header = jnp.stack([is_moved, cache_count])
        return (
            q_rows,
            bit_rows,
            cache_keys,
            cache_values,
            tree_keys[:tree_rows],
            tree_values[:tree_rows],
            header,
        )

    def attend_moved(parcel):
        q_rows, bit_rows, moved_keys, moved_values, moved_tree_keys, moved_tree_values, header = (
            parcel
        )

        def compute_block():
            tree_ok = unpack_bits(bit_rows)[:, : moved_tree_keys.shape[0]]
            return attend_rows(
                q_rows,
                tree_ok,
                moved_keys,
                moved_values,
                moved_tree_keys,
                moved_tree_values,
                header[1],
                sinks,
            ).astype(jnp.bfloat16)

        def empty_block():
            return jnp.zeros((block_size, QH * HD), jnp.bfloat16)

        return lax.cond(header[0] > 0, compute_block, empty_block)

    def put_back(result, rows_out, row_start, is_moved):
        current = lax.dynamic_slice_in_dim(result, row_start, block_size, 0)
        chosen_rows = jnp.where(is_moved > 0, rows_out, current)
        return lax.dynamic_update_slice_in_dim(result, chosen_rows, row_start, 0)

    parcel_x = make_parcel(start_x, send_x, tree_rows_x)
    parcel_y = make_parcel(start_y, send_y, node_total)
    got_x = passed_along(
        (parcel_x[0], parcel_x[1], parcel_x[2], parcel_x[3], parcel_x[4], parcel_x[5], parcel_x[6]),
        "gx",
        1,
    )
    got_y = passed_along(
        (parcel_y[0], parcel_y[1], parcel_y[2], parcel_y[3], parcel_y[4], parcel_y[5], parcel_y[6]),
        "gy",
        1,
    )
    result = lax.fori_loop(0, kept_blocks, home_step, result)
    done_x = attend_moved(got_x)
    done_y = attend_moved(got_y)
    returned_x = passed_along(done_x, "gx", -1)
    returned_y = passed_along(done_y, "gy", -1)
    result = put_back(result, returned_x, start_x, send_x)
    result = put_back(result, returned_y, start_y, send_y)
    node_live = jnp.arange(node_total, dtype=jnp.int32) < node_limit
    attended = jnp.where(node_live[:, None], result, jnp.zeros_like(result))
    projected = jnp.dot(
        attended,
        lax.all_gather(o_weight, ("gx", "gy"), axis=0, tiled=True),
        preferred_element_type=jnp.float32,
    )
    return (attended[None], projected.astype(jnp.bfloat16)[None])


def solution(mesh):
    placed = (
        P(("gx", "gy"), None, None),
        P(("gx", "gy"), None, None),
        P(("gx", "gy"), None, None),
        P(("gx", "gy"), None, None),
        P(("gx", "gy"), None, None),
        P(("gx", "gy"), None, None),
        P(("gx", "gy")),
        P(("gx", "gy")),
        P(),
        P(("gx", "gy"), None),
    )
    return jax.shard_map(
        on_device,
        mesh=mesh,
        in_specs=placed,
        out_specs=(P(("gx", "gy"), None, None), P(("gx", "gy"), None, None)),
        check_vma=False,
    )
```

profile of v0, /device:TPU:27, one launch (start us, length us, event | category | flops | bytes accessed | tf_op | source)
XLA Modules:
  0.0 608.0 jit_solution(9022590389764629002)
XLA Ops:
  17.5 70.6 %collective-permute-done = s32[2]{0:T(128)S(1)} collective-permute-done((s32[2]{0:T(128)S(1)}, s32[2]{0:T(128)S(1)}, u32[]{:S(2)}, u32[]{:S(2)}) %collective-permute-start) | collective-permute-done | bytes 40 | tf_op jit(solution)/shard_map/ppermute | solution.py:17
  97.3 9.7 %collective-permute-done.6 = bf16[384,512]{1,0:T(8,128)(2,1)} collective-permute-done((bf16[384,512]{1,0:T(8,128)(2,1)S(1)}, bf16[384,512]{1,0:T(8,128)(2,1)}, u32[]{:S(2)}, u32[]{:S(2)}) %collective-permute-start.6) | collective-permute-done | bytes 393248 | tf_op jit(solution)/shard_map/ppermute | solution.py:17
  111.8 22.1 %collective-permute-done.8 = s32[2]{0:T(128)S(1)} collective-permute-done((s32[2]{0:T(128)S(1)}, s32[2]{0:T(128)S(1)}, u32[]{:S(2)}, u32[]{:S(2)}) %collective-permute-start.8) | collective-permute-done | bytes 40 | tf_op jit(solution)/shard_map/ppermute | solution.py:17
  133.8 121.2 %collective-permute-start.10 = (bf16[128,4096]{1,0:T(8,128)(2,1)}, bf16[128,4096]{1,0:T(8,128)(2,1)}, u32[]{:S(2)}, u32[]{:S(2)}) collective-permute-start(bf16[128,4096]{1,0:T(8,128)(2,1)} %get-tuple-element.500), channel_id=1, source_target_pairs={{0,1},{1,2},{2,3},{3,4},{4,5},{5,6},{6,7},{7,0},{8,9},{9,10},{10,1... | collective-permute-start | bytes 3145736 | tf_op jit(solution)/shard_map/ppermute | solution.py:17
  255.1 4.5 collective-permute-start.7
  262.2 295.1 %while.44 = (s32[]{:T(128)}, bf16[512,4096]{1,0:T(8,128)(2,1)}, s32[]{:T(128)}, bf16[512,4096]{1,0:T(8,128)(2,1)}, s32[]{:T(128)}, /*index=5*/s32[512,16]{0,1:T(...) while((s32[]{:T(128)}, bf16[512,4096]{1,0:T(8,128)(2,1)}, ...), condition=%wide.region_7.8_spmd, body=%wide.region_0.7_spmd.sunk | while | flops 418252800 | bytes 47441316 | solution.py:169
  264.1 143.3 %while.45 = (s32[]{:T(128)}, bf16[8,128,512]{2,1,0:T(8,128)(2,1)}, s32[8]{0:T(128)S(1)}, bf16[128,4096]{1,0:T(8,128)(2,1)S(1)}, bf16[1024,512]{1,0:T(8,128)(2,1)...) while((s32[]{:T(128)}, bf16[8,128,512]{2,1,0:T(8,128)(2,1)}, ...), condition=%wide.region_6.6_spmd.clone, body=%wide.region_1.5_spmd.clone.sunk | while | flops 418056192 | bytes 40920024 | solution.py:71
  266.9 3.7 fusion.141
  284.8 3.7 fusion.141
  302.8 3.7 fusion.141
  320.7 3.7 fusion.141
  338.6 3.7 fusion.141
  356.5 3.7 fusion.141
  374.4 3.7 fusion.141
  392.3 3.7 fusion.141
  411.5 143.3 %while.45 = (s32[]{:T(128)}, bf16[8,128,512]{2,1,0:T(8,128)(2,1)}, s32[8]{0:T(128)S(1)}, bf16[128,4096]{1,0:T(8,128)(2,1)S(1)}, bf16[1024,512]{1,0:T(8,128)(2,1)...) while((s32[]{:T(128)}, bf16[8,128,512]{2,1,0:T(8,128)(2,1)}, ...), condition=%wide.region_6.6_spmd.clone, body=%wide.region_1.5_spmd.clone.sunk | while | flops 418056192 | bytes 40920024 | solution.py:71
  432.2 3.7 fusion.141
  468.1 3.7 fusion.141
  486.0 3.7 fusion.141
  503.9 3.7 fusion.141
  521.8 3.7 fusion.141
  561.1 13.2 %collective-permute-done.15 = bf16[128,4096]{1,0:T(8,128)(2,1)S(1)} collective-permute-done((bf16[128,4096]{1,0:T(8,128)(2,1)S(1)}, bf16[128,4096]{1,0:T(8,128)(2,1)S(1)}, u32[]{:S(2)}, u32[]{:S(2)}) %collective-permute-start.15) | collective-permute-done | bytes 1048608 | tf_op jit(solution)/shard_map/ppermute | solution.py:17
  576.8 4.5 fusion.85
  581.4 19.8 %fusion.84 = bf16[1,512,2880]{1,2,0:T(8,128)(2,1)} fusion(bf16[4096,2880]{0,1:T(8,128)(2,1)} %all-gather.2.cloned.1.call-done, bf16[512,4096]{1,0:T(8,128)(2,1)} %select_dynamic-update-slice_fusion, pred[512]{0:T(512)(128)(4,1)S(1)} %iota_compare_fusion.3), kind=kOutput, calls=%fused_computation.116 | convolution fusion | flops 12083167232 | bytes 30736896 | tf_op jit(solution)/shard_map/dot_general | solution.py:178
  (412 shorter events, 246.8 us)
Async XLA Ops:
  7.2 10.4 %copy-start.4 = (s32[1,512,16]{1,2,0:T(8,128)S(1)}, s32[1,512,16]{1,2,0:T(8,128)}, u32[]{:S(2)}) copy-start(s32[1,512,16]{1,2,0:T(8,128)} %param.27) | copy-start | bytes 98308
  7.2 103.5 %copy-start.6 = (f32[64]{0:T(128)S(1)}, f32[64]{0:T(128)}, u32[]{:S(2)}) copy-start(f32[64]{0:T(128)} %param.30) | copy-start | bytes 772
  7.2 574.2 %all-gather.2.cloned.1.call-start = ((), (), s32[]{:S(2)}) async-start(), calls=%async_computation | async-start | bytes 24330240 | tf_op jit(solution)/shard_map/all_gather | solution.py:180
  10.6 97.5 %collective-permute-start.2 = (bf16[128,4096]{1,0:T(8,128)(2,1)S(1)}, bf16[128,4096]{1,0:T(8,128)(2,1)}, u32[]{:S(2)}, u32[]{:S(2)}) collective-permute-start(bf16[128,4096]{1,0:T(8,128)(2,1)S(1)} %get-tuple-element.501), channel_id=1, source_target_pairs={{0,8},{8,16},{16,24},{24,0},{1,9},{9,17},{17,25},{25,1},{2,10},{10... | collective-permute-start | bytes 3145736 | tf_op jit(solution)/shard_map/ppermute | solution.py:17
  11.9 98.6 %collective-permute-start.3 = (bf16[1024,512]{1,0:T(8,128)(2,1)}, bf16[1024,512]{1,0:T(8,128)(2,1)S(1)}, u32[]{:S(2)}, u32[]{:S(2)}) collective-permute-start(bf16[1024,512]{1,0:T(8,128)(2,1)} %bitcast.12), channel_id=1, source_target_pairs={{0,8},{8,16},{16,24},{24,0},{1,9},{9,17},{17,25},{25,1},{2,10},{10... | collective-permute-start | bytes 3145736 | tf_op jit(solution)/shard_map/ppermute | solution.py:17
  13.0 97.5 %collective-permute-start.5 = (bf16[1024,512]{1,0:T(8,128)(2,1)}, bf16[1024,512]{1,0:T(8,128)(2,1)}, u32[]{:S(2)}, u32[]{:S(2)}) collective-permute-start(bf16[1024,512]{1,0:T(8,128)(2,1)} %bitcast.14), channel_id=1, source_target_pairs={{0,8},{8,16},{16,24},{24,0},{1,9},{9,17},{17,25},{25,1},{2,10},{10... | collective-permute-start | bytes 3145736 | tf_op jit(solution)/shard_map/ppermute | solution.py:17
  14.3 80.0 %collective-permute-start.4 = (bf16[384,512]{1,0:T(8,128)(2,1)S(1)}, bf16[384,512]{1,0:T(8,128)(2,1)}, u32[]{:S(2)}, u32[]{:S(2)}) collective-permute-start(bf16[384,512]{1,0:T(8,128)(2,1)S(1)} %slice_bitcast_fusion.1), channel_id=1, source_target_pairs={{0,8},{8,16},{16,24},{24,0},{1,9},{9,17},{17,25},{25,1},{2,10},{10... | collective-permute-start | bytes 1179656 | tf_op jit(solution)/shard_map/ppermute | solution.py:17
  16.3 71.8 %collective-permute-start = (s32[2]{0:T(128)S(1)}, s32[2]{0:T(128)S(1)}, u32[]{:S(2)}, u32[]{:S(2)}) collective-permute-start(s32[2]{0:T(128)S(1)} %pad_add_fusion), channel_id=1, source_target_pairs={{0,8},{8,16},{16,24},{24,0},{1,9},{9,17},{17,25},{25,1},{2,10},{10... | collective-permute-start | bytes 32 | tf_op jit(solution)/shard_map/ppermute | solution.py:17
  88.1 3.1 collective-permute-start.1
  91.2 164.0 %collective-permute-start.12 = (bf16[512,512]{1,0:T(8,128)(2,1)}, bf16[512,512]{1,0:T(8,128)(2,1)S(1)}, u32[]{:S(2)}, u32[]{:S(2)}) collective-permute-start(bf16[512,512]{1,0:T(8,128)(2,1)} %bitcast.13), channel_id=1, source_target_pairs={{0,1},{1,2},{2,3},{3,4},{4,5},{5,6},{6,7},{7,0},{8,9},{9,10},{10,1... | collective-permute-start | bytes 1572872 | tf_op jit(solution)/shard_map/ppermute | solution.py:17
  94.3 12.6 %collective-permute-start.6 = (bf16[384,512]{1,0:T(8,128)(2,1)S(1)}, bf16[384,512]{1,0:T(8,128)(2,1)}, u32[]{:S(2)}, u32[]{:S(2)}) collective-permute-start(bf16[384,512]{1,0:T(8,128)(2,1)S(1)} %slice_bitcast_fusion), channel_id=1, source_target_pairs={{0,8},{8,16},{16,24},{24,0},{1,9},{9,17},{17,25},{25,1},{2,10},{10... | collective-permute-start | bytes 1179656 | tf_op jit(solution)/shard_map/ppermute | solution.py:17
  107.0 148.1 %collective-permute-start.9 = (s32[128,16]{0,1:T(8,128)S(1)}, s32[128,16]{0,1:T(8,128)S(1)}, u32[]{:S(2)}, u32[]{:S(2)}) collective-permute-start(s32[128,16]{0,1:T(8,128)S(1)} %get-tuple-element.502), channel_id=1, source_target_pairs={{0,1},{1,2},{2,3},{3,4},{4,5},{5,6},{6,7},{7,0},{8,9},{9,10},{10,1... | collective-permute-start | bytes 24584 | tf_op jit(solution)/shard_map/ppermute | solution.py:17
  108.2 449.7 %collective-permute-start.11 = (bf16[1024,512]{1,0:T(8,128)(2,1)}, bf16[1024,512]{1,0:T(8,128)(2,1)}, u32[]{:S(2)}, u32[]{:S(2)}) collective-permute-start(bf16[1024,512]{1,0:T(8,128)(2,1)} %bitcast.12), channel_id=1, source_target_pairs={{0,1},{1,2},{2,3},{3,4},{4,5},{5,6},{6,7},{7,0},{8,9},{9,10},{10,1... | collective-permute-start | bytes 3145736 | tf_op jit(solution)/shard_map/ppermute | solution.py:17
  110.5 447.4 %collective-permute-start.13 = (bf16[1024,512]{1,0:T(8,128)(2,1)}, bf16[1024,512]{1,0:T(8,128)(2,1)}, u32[]{:S(2)}, u32[]{:S(2)}) collective-permute-start(bf16[1024,512]{1,0:T(8,128)(2,1)} %bitcast.14), channel_id=1, source_target_pairs={{0,1},{1,2},{2,3},{3,4},{4,5},{5,6},{6,7},{7,0},{8,9},{9,10},{10,1... | collective-permute-start | bytes 3145736 | tf_op jit(solution)/shard_map/ppermute | solution.py:17
  110.6 23.3 %collective-permute-start.8 = (s32[2]{0:T(128)S(1)}, s32[2]{0:T(128)S(1)}, u32[]{:S(2)}, u32[]{:S(2)}) collective-permute-start(s32[2]{0:T(128)S(1)} %pad_add_fusion.1), channel_id=1, source_target_pairs={{0,1},{1,2},{2,3},{3,4},{4,5},{5,6},{6,7},{7,0},{8,9},{9,10},{10,1... | collective-permute-start | bytes 32 | tf_op jit(solution)/shard_map/ppermute | solution.py:17
  133.8 128.3 %copy-start.7 = (s32[2]{0:T(128)}, s32[2]{0:T(128)S(1)}, u32[]{:S(2)}) copy-start(s32[2]{0:T(128)S(1)} %collective-permute-done.8) | copy-start | bytes 28
  133.8 424.0 %collective-permute-start.10 = (bf16[128,4096]{1,0:T(8,128)(2,1)}, bf16[128,4096]{1,0:T(8,128)(2,1)}, u32[]{:S(2)}, u32[]{:S(2)}) collective-permute-start(bf16[128,4096]{1,0:T(8,128)(2,1)} %get-tuple-element.500), channel_id=1, source_target_pairs={{0,1},{1,2},{2,3},{3,4},{4,5},{5,6},{6,7},{7,0},{8,9},{9,10},{10,1... | collective-permute-start | bytes 3145736 | tf_op jit(solution)/shard_map/ppermute | solution.py:17
  255.1 7.1 %copy-start.5 = (s32[128,16]{0,1:T(8,128)}, s32[128,16]{0,1:T(8,128)S(1)}, u32[]{:S(2)}) copy-start(s32[128,16]{0,1:T(8,128)S(1)} %collective-permute-done.9) | copy-start | bytes 24580
  255.1 302.8 %collective-permute-start.14 = (bf16[512,512]{1,0:T(8,128)(2,1)}, bf16[512,512]{1,0:T(8,128)(2,1)}, u32[]{:S(2)}, u32[]{:S(2)}) collective-permute-start(bf16[512,512]{1,0:T(8,128)(2,1)} %bitcast.15), channel_id=1, source_target_pairs={{0,1},{1,2},{2,3},{3,4},{4,5},{5,6},{6,7},{7,0},{8,9},{9,10},{10,1... | collective-permute-start | bytes 1572872 | tf_op jit(solution)/shard_map/ppermute | solution.py:17
  255.1 7.0 %copy-start.3 = (bf16[512,512]{1,0:T(8,128)(2,1)}, bf16[512,512]{1,0:T(8,128)(2,1)S(1)}, u32[]{:S(2)}) copy-start(bf16[512,512]{1,0:T(8,128)(2,1)S(1)} %collective-permute-done.12) | copy-start | bytes 1572868
  255.1 303.2 %collective-permute-start.7 = (bf16[128,4096]{1,0:T(8,128)(2,1)}, bf16[128,4096]{1,0:T(8,128)(2,1)}, u32[]{:S(2)}, u32[]{:S(2)}) collective-permute-start(bf16[128,4096]{1,0:T(8,128)(2,1)} %get-tuple-element.1062), channel_id=1, source_target_pairs={{0,24},{8,0},{16,8},{24,16},{1,25},{9,1},{17,9},{25,17},{2,26},{10... | collective-permute-start | bytes 3145736 | tf_op jit(solution)/shard_map/ppermute | solution.py:17
  327.6 3.6 copy-start
  381.3 3.6 copy-start
  558.0 16.3 %collective-permute-start.15 = (bf16[128,4096]{1,0:T(8,128)(2,1)S(1)}, bf16[128,4096]{1,0:T(8,128)(2,1)S(1)}, u32[]{:S(2)}, u32[]{:S(2)}) collective-permute-start(bf16[128,4096]{1,0:T(8,128)(2,1)S(1)} %get-tuple-element.1063), channel_id=1, source_target_pairs={{0,7},{1,0},{2,1},{3,2},{4,3},{5,4},{6,5},{7,6},{8,15},{9,8},{10,9... | collective-permute-start | bytes 3145736 | tf_op jit(solution)/shard_map/ppermute | solution.py:17
  (14 other events, 50.7 us)
Sparse Core Ops, SparseCore 0:
  97.4 162.8 all-gather.1
where the time goes:
time: 612 us; the launch traced here: 608 us
  matrix products  159 us (26%)
  starting transfers between devices  142 us (23%)
  waiting for transfers between devices  116 us (19%)
  other arithmetic  78.2 us (13%)
  local copies, waits for them, and re-layouts  63.4 us (10%)
  loops' own time  32.4 us (5%)
  between operations  16.1 us (3%)
    ppermute x16, starting transfers between devices, passed_along(): lax.ppermute(x, axis, [(i, (i + by) % length) for i in range(length)])  142 us
    ppermute x16, waiting for transfers between devices, passed_along(): lax.ppermute(x, axis, [(i, (i + by) % length) for i in range(length)])  116 us
    dot_general x16, matrix products, per_kv_head(): jnp.dot(q_part, key_cache.T, preferred_element_type=jnp.float32)  59.6 us
    reduce_sum x16, other arithmetic, per_kv_head(): jnp.sum(weight_cache, axis=1)  52 us
    dot_general x16, matrix products, per_kv_head(): jnp.dot(weight_cache.astype(jnp.bfloat16), value_cache, preferred_element...  34 us
    another operation x2, loops' own time, attend_rows(): per_head = lax.map(per_kv_head, jnp.arange(KVH, dtype=jnp.int32))  32.1 us
    dot_general x16, matrix products, per_kv_head(): jnp.dot(q_part, key_tree.T, preferred_element_type=jnp.float32)  23.6 us
    dot_general x16, matrix products, per_kv_head(): jnp.dot(weight_tree.astype(jnp.bfloat16), value_tree, preferred_element_t...  22.4 us
  transfers between devices with their start and end apart: 17, of which 5 were waited for; matrix products, arithmetic and copies ran while one was open for 46% of the time, Pallas kernels for 0%

commit v1 on v0

v1 whole, which is shorter than its diff:
```python
import functools

import jax
import jax.numpy as jnp
from jax import lax
from jax.experimental import pallas as pl
from jax.experimental.pallas import tpu as pltpu
from jax.sharding import PartitionSpec as P

QH = 64
KVH = 8
HD = 64
BLK = 128
PAIRS = QH // KVH // 2
MASKED = -1e30
MESH = pl.DeviceIdType.MESH


def gray(r, size):
    out, bit = 0, 1
    while bit < size:
        out = out + ((r // bit) % 2 + (r // (2 * bit)) % 2) % 2 * bit
        bit *= 2
    return out


def ungray(g, size):
    out, bit = 0, 1
    while bit < size:
        total, top = 0, bit
        while top < size:
            total = total + (g // top) % 2
            top *= 2
        out = out + total % 2 * bit
        bit *= 2
    return out


def kernel(
    R, L,
    q_h, kc_h, vc_h, kt_h, vt_h, bits_ref, nc_ref, cl_ref, sinks_ref, w_h,
    att_h, proj_h, wfull,
    w_own, q_v, k_v, v_v, kk, vv, bias, att_v, acc, wbuf, proj_v,
    line_send, line_recv, ring_send, ring_recv, d2d_send, d2d_recv, load_sem, wb_sem, own_sem, out_sem,
):
    gx, gy = lax.axis_index("gx"), lax.axis_index("gy")
    core, z = gy % 2, gy // 2
    r = ungray(gx, R)
    rows = w_own.shape[0]
    half = rows // 2
    nodes = q_v.shape[0]
    cache = kc_h.shape[0]
    busy = (gx + gy) % 2 == 0

    def dev(rr, zz, cc):
        return (gray(rr % R, R), 2 * zz + cc)

    def row_of(rr, zz, cc, h=0):
        return pl.multiple_of((gray(rr % R, R) * 2 * L + 2 * zz + cc) * rows + h * half, 16)

    right, left = dev(r + 1, z, core), dev(r + R - 1, z, core)
    partner = (gx, 2 * z + 1 - core)

    barrier = pltpu.get_barrier_semaphore()
    for nb in (right, left, partner):
        pl.semaphore_signal(barrier, inc=1, device_id=nb, device_id_type=MESH)

    @pl.when(z > 0)
    def _():
        pl.semaphore_signal(barrier, inc=1, device_id=(gx, gy - 2), device_id_type=MESH)

    @pl.when(z < L - 1)
    def _():
        pl.semaphore_signal(barrier, inc=1, device_id=(gx, gy + 2), device_id_type=MESH)

    own_load = pltpu.make_async_copy(w_h, w_own, own_sem.at[0])
    own_load.start()
    loads = [
        pltpu.make_async_copy(q_h, q_v, load_sem.at[0]),
        pltpu.make_async_copy(kc_h, k_v.at[pl.ds(0, cache)], load_sem.at[1]),
        pltpu.make_async_copy(vc_h, v_v.at[pl.ds(0, cache)], load_sem.at[2]),
        pltpu.make_async_copy(kt_h, k_v.at[pl.ds(cache, nodes)], load_sem.at[3]),
        pltpu.make_async_copy(vt_h, v_v.at[pl.ds(cache, nodes)], load_sem.at[4]),
    ]
    for c in loads:
        c.start()
    pl.semaphore_wait(barrier, 3 + jnp.minimum(z, 1) + jnp.minimum(L - 1 - z, 1))
    own_load.wait()

    def piece(rr, zz, cc, h):
        return wfull.at[pl.ds(row_of(rr, zz, cc, h), half)]

    def line_copy(src, zz, up):
        d = 0 if up else 1
        return pltpu.make_async_remote_copy(
            src_ref=src, dst_ref=wfull.at[pl.ds(row_of(r, zz, core), rows)],
            send_sem=line_send.at[d, zz], recv_sem=line_recv.at[zz],
            device_id=(gx, gy + 2 if up else gy - 2), device_id_type=MESH,
        )

    def ring_copy(src, rr, zz, h):
        return pltpu.make_async_remote_copy(
            src_ref=src, dst_ref=piece(rr, zz, core, h),
            send_sem=ring_send.at[h, rr, zz], recv_sem=ring_recv.at[h, rr, zz],
            device_id=left if h else right, device_id_type=MESH,
        )

    def d2d_copy(src, rr, zz, h, cc=None):
        return pltpu.make_async_remote_copy(
            src_ref=src, dst_ref=piece(rr, zz, core if cc is None else cc, h),
            send_sem=d2d_send.at[h, rr, zz], recv_sem=d2d_recv.at[h, rr, zz],
            device_id=partner, device_id_type=MESH,
        )

    @pl.when(z < L - 1)
    def _():
        line_copy(w_own, z, True).start()

    @pl.when(z > 0)
    def _():
        line_copy(w_own, z, False).start()

    for h in range(2):
        ring_copy(w_own.at[pl.ds(h * half, half)], r, z, h).start()
    for h in range(2):
        d2d_copy(w_own.at[pl.ds(h * half, half)], r, z, h).start()
    own_store = pltpu.make_async_copy(w_own, wfull.at[pl.ds(row_of(r, z, core), rows)], own_sem.at[1])
    own_store.start()

    def z_at(t):
        m = jnp.minimum(z, L - 1 - z)
        k = (t + 1) // 2
        near = z + k * (2 * (t % 2) - 1)
        far = jnp.where(z < L - 1 - z, z + t - m, z - t + m)
        return jnp.where(t <= 2 * m, near, far)

    def line_event(t):
        zz = z_at(t)
        share = wfull.at[pl.ds(row_of(r, zz, core), rows)]
        line_copy(share, zz, True).wait_recv()

        @pl.when(jnp.logical_and(zz < z, z < L - 1))
        def _():
            line_copy(share, zz, True).start()

        @pl.when(jnp.logical_and(zz > z, z > 0))
        def _():
            line_copy(share, zz, False).start()

        for h in range(2):
            ring_copy(piece(r, zz, core, h), r, zz, h).start()
        for h in range(2):
            d2d_copy(piece(r, zz, core, h), r, zz, h).start()

    def service(e):
        t = e // (R - 1)
        j = e % (R - 1) + 1

        @pl.when(jnp.logical_and(j == min(2, R - 1), t + 1 < L))
        def _():
            line_event(t + 1)

        zz = z_at(t)
        for h in range(2):
            rr = (r + j if h else r + R - j) % R
            here = piece(rr, zz, core, h)
            ring_copy(here, rr, zz, h).wait_recv()

            @pl.when(j < R - 1)
            def _():
                ring_copy(here, rr, zz, h).start()

            d2d_copy(here, rr, zz, h).start()

    events = L * (R - 1)

    lane = lax.broadcasted_iota(jnp.int32, (nodes, 128), 1)
    for t in range(nodes // 128):
        word = bits_ref[:, 4 * t + 3 : 4 * t + 4]
        for w in (2, 1, 0):
            word = jnp.where(lane < 32 * (w + 1), bits_ref[:, 4 * t + w : 4 * t + w + 1], word)
        flag = jnp.bitwise_and(jnp.right_shift(word, lane % 32), 1)
        bias[:, t * 128 : (t + 1) * 128] = jnp.where(flag > 0, 0.0, MASKED).astype(jnp.float32)

    @pl.when(jnp.logical_not(busy))
    def _():
        att_v[...] = jnp.zeros_like(att_v)

    for c in loads:
        c.wait()

    total = cache + nodes
    key_id = lax.broadcasted_iota(jnp.int32, (total, 128), 0)
    key_ok = jnp.logical_or(key_id < cl_ref[0], key_id >= cache)
    low = lax.broadcasted_iota(jnp.int32, (total, 128), 1) < HD
    ones = jnp.where(key_ok, 1.0, 0.0)
    vv[0, :, 128:] = jnp.where(low, ones, 0.0).astype(jnp.bfloat16)
    vv[1, :, 128:] = jnp.where(low, 0.0, ones).astype(jnp.bfloat16)

    def prepare(g):
        col = pl.ds(pl.multiple_of(g // 2 * 128, 128), 128)
        for src, dst, gain in ((k_v, kk, HD**-0.5), (v_v, vv, 1.0)):
            x = src[:, col].astype(jnp.float32) * gain
            x = jnp.where(key_ok, x, 0.0)
            y = pltpu.roll(x, HD, 1)
            even = (g + jnp.zeros_like(key_id)) % 2 == 0
            dst[0, :, :128] = jnp.where(low, jnp.where(even, x, y), 0.0).astype(jnp.bfloat16)
            dst[1, :, :128] = jnp.where(low, 0.0, jnp.where(even, y, x)).astype(jnp.bfloat16)

    def unit(g, i):
        first = i * BLK
        keys = cache + first + BLK
        qs = jnp.concatenate(
            [
                q_v[first : first + BLK, pl.ds(pl.multiple_of(g * 2 * PAIRS * HD + p * 128, 128), 128)]
                for p in range(PAIRS)
            ],
            axis=0,
        )
        mask = bias[first : first + BLK, : first + BLK]
        mask = jnp.concatenate([mask] * PAIRS, axis=0)
        out, extra = None, []
        for h in range(2):
            s = lax.dot_general(
                qs, kk[h, :keys, :], (((1,), (1,)), ((), ())), preferred_element_type=jnp.float32
            )
            s_tree = s[:, cache:] + mask
            s_cache = s[:, :cache]
            sink = jnp.concatenate(
                [jnp.full((BLK, 1), sinks_ref[g * 2 * PAIRS + 2 * p + h], jnp.float32) for p in range(PAIRS)],
                axis=0,
            )
            top = jnp.maximum(
                sink,
                jnp.maximum(
                    jnp.max(s_cache, axis=1, keepdims=True), jnp.max(s_tree, axis=1, keepdims=True)
                ),
            )
            p_cache = jnp.exp(s_cache - top).astype(jnp.bfloat16)
            p_tree = jnp.exp(s_tree - top).astype(jnp.bfloat16)
            o = jnp.dot(p_cache, vv[h, :cache, :], preferred_element_type=jnp.float32)
            o = o + jnp.dot(p_tree, vv[h, cache:keys, :], preferred_element_type=jnp.float32)
            out = o if out is None else out + o
            extra.append(jnp.exp(sink - top))
        lanes = lax.broadcasted_iota(jnp.int32, (PAIRS * BLK, 128), 1)
        den = out[:, 128:] + jnp.where(lanes < HD, extra[0], extra[1])
        res = out[:, :128] / den
        row = lax.broadcasted_iota(jnp.int32, (BLK, 128), 0) + first
        for p in range(PAIRS):
            part = jnp.where(row < nc_ref[0], res[p * BLK : (p + 1) * BLK], 0.0)
            att_v[
                first : first + BLK, pl.ds(pl.multiple_of(g * 2 * PAIRS * HD + p * 128, 128), 128)
            ] = part.astype(jnp.bfloat16)

    early = min(KVH, events)

    def head_step(g, carry):
        prepare(g)
        unit(g, 0)

        @pl.when(busy)
        def _():
            for i in range(1, nodes // BLK):
                unit(g, i)

        @pl.when(g < early)
        def _():
            service(g)

        return carry

    lax.fori_loop(0, KVH, head_step, 0)
    att_store = pltpu.make_async_copy(att_v, att_h, out_sem.at[0])
    att_store.start()
    own_store.wait()
    acc[...] = jnp.zeros_like(acc)

    def chunk_load(rr, zz):
        return pltpu.make_async_copy(
            wfull.at[pl.ds(row_of(rr, zz, 0), 2 * rows)], wbuf.at[rr % 2], wb_sem.at[rr % 2]
        )

    def project(t):
        zz = z_at(t)
        for h in range(2):
            for rr in range(R):
                d2d_copy(piece(rr, zz, core, h), rr, zz, h, 1 - core).wait_recv()
        chunk_load(0, zz).start()
        for rr in range(R):
            if rr + 1 < R:
                chunk_load(rr + 1, zz).start()
            chunk_load(rr, zz).wait()
            a = att_v[:, pl.ds(row_of(rr, zz, 0), 2 * rows)] if (2 * rows) % 128 == 0 else None
            if a is None:
                base = row_of(rr, zz, 0)
                wide = att_v[:, pl.ds(pl.multiple_of(base // 128 * 128, 128), 128)]
                col = lax.broadcasted_iota(jnp.int32, (128, 2 * rows), 0)
                pick = col == base % 128 + lax.broadcasted_iota(jnp.int32, (128, 2 * rows), 1)
                a = jnp.dot(
                    wide, jnp.where(pick, 1.0, 0.0).astype(jnp.bfloat16), preferred_element_type=jnp.float32
                ).astype(jnp.bfloat16)
            acc[...] += jnp.dot(a, wbuf[rr % 2], preferred_element_type=jnp.float32)

    def project_step(t, carry):
        def late(e, c):
            service(e)
            return c

        lax.fori_loop(jnp.maximum(t * (R - 1), early), jnp.maximum((t + 1) * (R - 1), early), late, 0)
        project(t)
        return carry

    lax.fori_loop(0, L, project_step, 0)
    proj_v[...] = acc[...].astype(jnp.bfloat16)
    proj_store = pltpu.make_async_copy(proj_v, proj_h, out_sem.at[1])
    proj_store.start()

    def drain(zz, carry):
        @pl.when(jnp.logical_and(zz <= z, z < L - 1))
        def _():
            line_copy(w_own, zz, True).wait_send()

        @pl.when(jnp.logical_and(zz >= z, z > 0))
        def _():
            line_copy(w_own, zz, False).wait_send()

        for h in range(2):
            for j in range(R - 1):
                rr = (r + j if h else r + R - j) % R
                ring_copy(piece(rr, zz, core, h), rr, zz, h).wait_send()
            for rr in range(R):
                d2d_copy(piece(rr, zz, core, h), rr, zz, h).wait_send()
        return carry

    lax.fori_loop(0, L, drain, 0)
    att_store.wait()
    proj_store.wait()


def solution(mesh):
    R, L = mesh.shape["gx"], mesh.shape["gy"] // 2

    def on_device(q, kc, vc, kt, vt, bits, nc, cl, sinks, w):
        nodes, width = q.shape[1:]
        cache, kvw = kc.shape[1:]
        rows, d = w.shape
        total = cache + nodes
        bf, f32 = jnp.bfloat16, jnp.float32
        hbm = pl.BlockSpec(memory_space=pl.ANY)
        smem = pl.BlockSpec(memory_space=pltpu.SMEM)
        dma = pltpu.SemaphoreType.DMA
        att, proj, _ = pl.pallas_call(
            functools.partial(kernel, R, L),
            out_shape=(
                jax.ShapeDtypeStruct((nodes, width), bf),
                jax.ShapeDtypeStruct((nodes, d), bf),
                jax.ShapeDtypeStruct((width, d), bf),
            ),
            in_specs=[hbm] * 5 + [pl.BlockSpec(memory_space=pltpu.VMEM), smem, smem, smem, hbm],
            out_specs=(hbm, hbm, hbm),
            scratch_shapes=[
                pltpu.VMEM((rows, d), bf),
                pltpu.VMEM((nodes, width), bf),
                pltpu.VMEM((total, kvw), bf),
                pltpu.VMEM((total, kvw), bf),
                pltpu.VMEM((2, total, 128), bf),
                pltpu.VMEM((2, total, 256), bf),
                pltpu.VMEM((nodes, nodes), f32),
                pltpu.VMEM((nodes, width), bf),
                pltpu.VMEM((nodes, d), f32),
                pltpu.VMEM((2, 2 * rows, d), bf),
                pltpu.VMEM((nodes, d), bf),
                dma((2, L)), dma((L,)), dma((2, R, L)), dma((2, R, L)), dma((2, R, L)), dma((2, R, L)),
                dma((5,)), dma((2,)), dma((2,)), dma((2,)),
            ],
            compiler_params=pltpu.CompilerParams(
                collective_id=0, has_side_effects=True, vmem_limit_bytes=60 * 1024 * 1024
            ),
        )(q[0], kc[0], vc[0], kt[0], vt[0], bits[0], nc, cl, sinks, w)
        return att[None], proj[None]

    both = ("gx", "gy")
    cube = P(both, None, None)
    return jax.shard_map(
        on_device,
        mesh=mesh,
        in_specs=(cube,) * 6 + (P(both), P(both), P(), P(both, None)),
        out_specs=(cube, cube),
        check_vma=False,
    )
```

time: 612 us -> 175 us (0.29)
  matrix products: 159 us -> 0 us
  Pallas kernels: 0 us -> 157 us
  starting transfers between devices: 142 us -> 0 us
  waiting for transfers between devices: 116 us -> 0 us
  other arithmetic: 78.2 us -> 0 us
  local copies, waits for them, and re-layouts: 63.4 us -> 13.1 us
  loops' own time: 32.4 us -> 0 us
  between operations: 16.1 us -> 1.93 us
    dot_general x65 -> x0, matrix products: 159 us -> none  [the longest x16 59.6 us: per_kv_head(): jnp.dot(q_part, key_cache.T, preferred_element_type=jnp.float32)]
    pallas_call x0 -> x1, Pallas kernels: none -> 157 us  [on_device(): pl.pallas_call(functools.partial(kernel, R, L), out_shape=(jax.ShapeDtype...]
    ppermute x16 -> x0, starting transfers between devices: 142 us -> none  [passed_along(): lax.ppermute(x, axis, [(i, (i + by) % length) for i in range(length)])]
    ppermute x16 -> x0, waiting for transfers between devices: 116 us -> none  [passed_along(): lax.ppermute(x, axis, [(i, (i + by) % length) for i in range(length)])]
    reduce_sum x32 -> x0, other arithmetic: 57.2 us -> none  [the longest x16 52 us: per_kv_head(): jnp.sum(weight_cache, axis=1)]
    another operation x5 -> x0, loops' own time: 32.4 us -> none  [the longest x2 32.1 us: attend_rows(): per_head = lax.map(per_kv_head, jnp.arange(KVH, dtype=jnp.int32))]
    dynamic_slice x54 -> x0, local copies, waits for them, and re-layouts: 17.1 us -> none  [the longest x16 10.3 us: attend_rows(): per_head = lax.map(per_kv_head, jnp.arange(KVH, dtype=jnp.int32))]
    reshape x48 -> x0, local copies, waits for them, and re-layouts: 16.6 us -> none  [the longest x32 13.7 us: attend_rows(): tree_mask = jnp.repeat(tree_ok, groups, axis=0)]
  transfers between devices with their start and end apart: 17 -> 0, of which waited for: 5 -> 0; matrix products, arithmetic and copies ran while one was open for 46% -> 0% of each run, Pallas kernels for 0% -> 0%
where the time goes in v1:
time: 175 us; the launch traced here: 172 us
  Pallas kernels  157 us (90%)
  local copies, waits for them, and re-layouts  13.1 us (7%)
  between operations  1.93 us (1%)
    pallas_call x1, Pallas kernels, on_device(): pl.pallas_call(functools.partial(kernel, R, L), out_shape=(jax.ShapeDtype...  157 us
    unnamed x4, local copies, waits for them, and re-layouts  13.1 us

profile of v1, /device:TPU:27, one launch (start us, length us, event | category | flops | bytes accessed | tf_op | source)
XLA Modules:
  0.0 171.7 jit_solution(12823754333546166305)
XLA Ops:
  1.9 1.6 copy.12
  3.5 2.3 %copy.13.w_h = bf16[128,2880]{1,0:T(8,128)(2,1)} copy(bf16[128,2880]{0,1:T(8,128)(2,1)} %param.19) | data formatting | bytes 1474560 | tf_op args[9]
  5.8 156.7 %shard_map.113 = (bf16[512,4096]{1,0:T(8,128)(2,1)}, bf16[512,2880]{1,0:T(8,128)(2,1)}, bf16[4096,2880]{1,0:T(8,128)(2,1)}) custom-call(bf16[512,4096]{1,0:T(8,128)(2,1)} %bitcast.8, bf16[1024,512]{1,0:T(8,128)(2,1)} %bitcast.11, bf16[1024,512]{1,0:T(8,128)(2,1)} %bitcast.12, bf16[512,512]{1,0:T(8,128)(2,1)} %bitcast.14, bf16[512,512]{1,0:T(8,128)(2,1)} %bitcast.15, ...), custom_call_target="tpu_custom_call" | custom-call | tf_op jit(solution)/shard_map/pallas_call | solution.py:352
  162.4 4.6 %copy.14 = bf16[1,512,2880]{1,2,0:T(8,128)(2,1)} copy(bf16[1,512,2880]{2,1,0:T(8,128)(2,1)} %bitcast.10) | data formatting | bytes 5898240
  167.0 4.7 %copy.18 = bf16[1,512,4096]{2,1,0:T(8,128)(2,1)} copy(bf16[1,512,4096]{2,1,0:T(8,128)(2,1)} %bitcast.9) | data formatting | bytes 8388608
